TPU v7x, 256 devices: a whole 4x4x8 slice. The times are simulated.
256 devices in a mesh: row: 16 (over z_hi, y, core), col: 16 (over x, z_lo).
Axes of the slice: x: 4, y: 4, z: 8 (z_hi: 2, z_lo: 4; z = z_hi * 4 + z_lo), core: 2. Of those that a mesh axis runs over, the one named last changes fastest.
Arguments:
- series: float32 [16384, 2048], P(('row', 'col'))
- lengths: int32 [16384], P(('row', 'col')), may hold values from 512 to 2048
- starts: int32 [16384], P(('row', 'col')), may hold values from 0 to 1536, as said below
Outputs:
- correlation: float32 [16384, 16384], P('row', 'col')
Inputs may be any that keep to these rules, and one draw needn't show every extreme that they name: starts[s] + lengths[s] <= 2048 for every series.
All inputs are finite; a program needn't handle non-finite values.
Results may differ from a plain program's by a relative error of at most 0.0012.
Values may be sent and summed in bfloat16 or wider, within the bound.
A program may use at most 64 MiB of HBM per device.

v0:
```python
import jax
import jax.numpy as jnp
from jax import lax
from jax.sharding import Mesh
from jax.sharding import PartitionSpec as P

ROW = ("row_0", "row_1", "row_2")
ROW_COL = ("row_0", "row_1", "row_2", "col")


def from_everyone(x, axis):
    copies = jnp.broadcast_to(x, (lax.axis_size(axis), *x.shape))
    return lax.all_to_all(copies, axis, split_axis=0, concat_axis=0, tiled=True)


def joined_along(pieces, dim):
    shape = list(pieces.shape[1:])
    shape[dim] *= pieces.shape[0]
    return jnp.moveaxis(pieces, 0, dim).reshape(shape)


def gather_axes(x, axes, dim):
    far, near = axes
    pieces = from_everyone(from_everyone(x, far), near)
    return joined_along(pieces.swapaxes(0, 1).reshape(-1, *x.shape), dim)


def normalize(series, lengths, starts):
    positions = jnp.arange(series.shape[1], dtype=jnp.int32)[None, :]
    inside = ((positions >= starts[:, None]) & (positions < (starts + lengths)[:, None])).astype(
        jnp.float32
    )
    valid_count = lengths.astype(jnp.float32)[:, None]
    average = jnp.sum(inside * series, axis=1, keepdims=True) / valid_count
    centered = inside * (series - average)
    variance = jnp.sum(centered * centered, axis=1, keepdims=True) / valid_count
    return (centered / jnp.sqrt(valid_count * (variance + 1e-06))).astype(jnp.bfloat16)


def gram_block(left_rows, right_rows):
    return lax.dot_general(
        left_rows, right_rows, (((1,), (1,)), ((), ())), preferred_element_type=jnp.float32
    )


def on_device(series, lengths, starts):
    normed = normalize(series, lengths, starts)
    rows_dev = normed.shape[0]
    steps_total = normed.shape[1]
    row_total = lax.axis_size(ROW)
    col_total = lax.axis_size("col")
    panels_per_row = col_total // row_total
    strided = gather_axes(normed, (("row_0", "row_1"), "row_2"), 0)
    outgoing = jnp.repeat(strided.reshape(row_total, rows_dev, steps_total), panels_per_row, axis=0)
    outgoing = outgoing.reshape(col_total * rows_dev, steps_total)
    regrouped = lax.all_to_all(outgoing, "col", split_axis=0, concat_axis=0, tiled=True)
    return gram_block(lax.all_gather(normed, "col", axis=0, tiled=True), regrouped)


def solution(mesh):
    split = Mesh(
        mesh.devices.reshape(2, 4, 2, mesh.shape["col"]), ("row_0", "row_1", "row_2", "col")
    )
    placed = (P(ROW_COL, None), P(ROW_COL), P(ROW_COL))
    return jax.shard_map(
        on_device, mesh=split, in_specs=placed, out_specs=P(ROW, "col"), check_vma=False
    )
```

profile of v0, /device:TPU:1, one launch (start us, length us, event | category | flops | bytes accessed | tf_op | source)
XLA Modules:
  0.0 267.5 jit_solution(15791824681232021595)
XLA Ops:
  6.5 0.7 add.10
  7.2 1.4 select_reduce_fusion
  8.6 0.7 convert_divide_fusion.1
  9.2 1.5 multiply_reduce_fusion
  10.8 0.7 multiply_sqrt_fusion
  11.4 1.4 divide_convert_fusion
  12.9 0.0 copy-start
  12.9 1.6 broadcast_in_dim.4
  14.5 11.6 %all-to-all-start = ((bf16[8,64,2048]{2,1,0:T(8,128)(2,1)}), bf16[8,64,2048]{2,1,0:T(8,128)(2,1)S(1)}, u32[]{:S(2)}, u32[]{:S(2)}) async-start(bf16[8,64,2048]{2,1,0:T(8,128)(2,1)} %broadcast_in_dim.4), calls=%async_computation | async-start | bytes 4194304 | tf_op jit(solution)/shard_map/all_to_all | solution.py:13
  26.1 0.0 all-gather.2.cloned.1.call-start
  26.1 0.0 copy-done
  26.1 0.7 all-gather.2.cloned.1.call-update
  26.8 41.4 %all-to-all-done = bf16[8,64,2048]{2,1,0:T(8,128)(2,1)S(1)} async-done(((bf16[8,64,2048]{2,1,0:T(8,128)(2,1)}), bf16[8,64,2048]{2,1,0:T(8,128)(2,1)S(1)}, u32[]{:S(2)}, u32[]{:S(2)}) %all-to-all-start) | async-done | bytes 2097184 | tf_op jit(solution)/shard_map/all_to_all | solution.py:13
  68.2 0.5 broadcast_in_dim.5
  68.8 12.9 %all_to_all.22 = bf16[2,8,64,2048]{3,2,1,0:T(8,128)(2,1)S(1)} all-to-all(bf16[2,8,64,2048]{3,2,1,0:T(8,128)(2,1)S(1)} %broadcast_in_dim.5), channel_id=1, replica_groups=mesh['row_0'=2,'row_1'=4,'row_2'=2,'col'=16] {'row_2'}, dimensions={0} | all-to-all | bytes 8388608 | tf_op jit(solution)/shard_map/all_to_all | solution.py:13
  81.6 2.3 copy.4
  83.9 50.3 %all-to-all-start.2 = ((bf16[16,64,2048]{2,1,0:T(8,128)(2,1)}), bf16[16,64,2048]{2,1,0:T(8,128)(2,1)}, u32[]{:S(2)}, u32[]{:S(2)}) async-start(bf16[16,64,2048]{2,1,0:T(8,128)(2,1)} %bitcast.6), calls=%async_computation.2 | async-start | bytes 8388608 | tf_op jit(solution)/shard_map/all_to_all | solution.py:56
  134.2 83.3 %all-gather.2.cloned.1.call-done = bf16[1024,2048]{1,0:T(8,128)(2,1)} async-done(((bf16[64,2048]{1,0:T(8,128)(2,1)}), bf16[1024,2048]{1,0:T(8,128)(2,1)}) %all-gather.2.cloned.1.call-update) | async-done | bytes 4194320 | tf_op jit(solution)/shard_map/all_gather | solution.py:57
  217.5 33.1 %all-to-all-done.2 = bf16[16,64,2048]{2,1,0:T(8,128)(2,1)} async-done(((bf16[16,64,2048]{2,1,0:T(8,128)(2,1)}), bf16[16,64,2048]{2,1,0:T(8,128)(2,1)}, u32[]{:S(2)}, u32[]{:S(2)}) %all-to-all-start.2) | async-done | bytes 4194336 | tf_op jit(solution)/shard_map/all_to_all | solution.py:56
  250.6 10.0 %fusion.1 = f32[1024,1024]{1,0:T(8,128)} fusion(bf16[1024,2048]{1,0:T(8,128)(2,1)} %all-gather.2.cloned.1.call-done, bf16[1024,2048]{1,0:T(8,128)(2,1)} %bitcast.2), kind=kOutput, calls=%fused_computation.10 | convolution fusion | flops 4294967296 | bytes 12582912 | tf_op jit(solution)/shard_map/dot_general | solution.py:41
Async XLA Ops:
  12.9 13.3 %copy-start = (bf16[64,2048]{1,0:T(8,128)(2,1)}, bf16[64,2048]{1,0:T(8,128)(2,1)S(1)}, u32[]{:S(2)}) copy-start(bf16[64,2048]{1,0:T(8,128)(2,1)S(1)} %divide_convert_fusion) | copy-start | bytes 786436
  14.5 53.8 %all-to-all-start = ((bf16[8,64,2048]{2,1,0:T(8,128)(2,1)}), bf16[8,64,2048]{2,1,0:T(8,128)(2,1)S(1)}, u32[]{:S(2)}, u32[]{:S(2)}) async-start(bf16[8,64,2048]{2,1,0:T(8,128)(2,1)} %broadcast_in_dim.4), calls=%async_computation | async-start | bytes 4194304 | tf_op jit(solution)/shard_map/all_to_all | solution.py:13
  26.1 191.5 %all-gather.2.cloned.1.call-start = ((), (), s32[]{:S(2)}) async-start(), calls=%async_computation.3 | async-start | bytes 4456448 | tf_op jit(solution)/shard_map/all_gather | solution.py:57
  83.9 166.7 %all-to-all-start.2 = ((bf16[16,64,2048]{2,1,0:T(8,128)(2,1)}), bf16[16,64,2048]{2,1,0:T(8,128)(2,1)}, u32[]{:S(2)}, u32[]{:S(2)}) async-start(bf16[16,64,2048]{2,1,0:T(8,128)(2,1)} %bitcast.6), calls=%async_computation.2 | async-start | bytes 8388608 | tf_op jit(solution)/shard_map/all_to_all | solution.py:56
Sparse Core Ops, SparseCore 0:
  28.7 188.8 all-gather.1
where the time goes:
time: 268 us; the launch traced here: 267 us
  waiting for transfers between devices  158 us (59%)
  starting transfers between devices  62 us (23%)
  between operations  13.4 us (5%)
  blocking collectives  12.9 us (5%)
  matrix products  10 us (4%)
  other arithmetic  6.31 us (2%)
  local copies, waits for them, and re-layouts  4.42 us (2%)
    all_gather x1, waiting for transfers between devices, on_device(): lax.all_gather(normed, 'col', axis=0, tiled=True)  83.3 us
    all_to_all x1, starting transfers between devices, on_device(): lax.all_to_all(outgoing, 'col', split_axis=0, concat_axis=0, tiled=True)  50.3 us
    all_to_all x1, waiting for transfers between devices, from_everyone(): return lax.all_to_all(copies, axis, split_axis=0, concat_axis=0, tiled=True)  41.4 us
    all_to_all x1, waiting for transfers between devices, on_device(): lax.all_to_all(outgoing, 'col', split_axis=0, concat_axis=0, tiled=True)  33.1 us
    all_to_all x1, blocking collectives, from_everyone(): return lax.all_to_all(copies, axis, split_axis=0, concat_axis=0, tiled=True)  12.9 us
    all_to_all x1, starting transfers between devices, from_everyone(): return lax.all_to_all(copies, axis, split_axis=0, concat_axis=0, tiled=True)  11.6 us
    dot_general x1, matrix products, gram_block(): lax.dot_general(left_rows, right_rows, (((1,), (1,)), ((), ())), preferre...  10 us
  transfers between devices with their start and end apart: 3, of which 3 were waited for; matrix products, arithmetic and copies ran while one was open for 1% of the time, Pallas kernels for 0%

commit v1 on v0

v1 whole, which is shorter than its diff:
```python
import jax
import jax.numpy as jnp
from jax import lax
from jax.experimental import pallas as pl
from jax.experimental.pallas import tpu as pltpu
from jax.sharding import PartitionSpec as P

MESH = pl.DeviceIdType.MESH


def normalize(series, lengths, starts):
    positions = jnp.arange(series.shape[1], dtype=jnp.int32)[None, :]
    inside = ((positions >= starts[:, None]) & (positions < (starts + lengths)[:, None])).astype(
        jnp.float32
    )
    valid_count = lengths.astype(jnp.float32)[:, None]
    average = jnp.sum(inside * series, axis=1, keepdims=True) / valid_count
    centered = inside * (series - average)
    variance = jnp.sum(centered * centered, axis=1, keepdims=True) / valid_count
    return (centered / jnp.sqrt(valid_count * (variance + 1e-06))).astype(jnp.bfloat16)


def exchange(own, out, rows, cols, send_sem, row_sem, col_sem):
    row, col = lax.axis_index("row"), lax.axis_index("col")
    half, y, core = row // 8, (row // 2) % 4, row % 2
    x, z = col // 4, col % 4
    right, left = (x + 1) % 4, (x + 3) % 4
    up, down = (y + 1) % 4, (y + 3) % 4

    def at_col(x_to, z_to):
        return (row, x_to * 4 + z_to)

    def at_y(y_to):
        return (half * 8 + y_to * 2 + core, col)

    sibling = (row + 1 - 2 * core, col)
    line = [at_col(x, (z + s) % 4) for s in (1, 2, 3)]
    sides = [at_col(right, z), at_col(left, z)]
    ring = [at_y(up), at_y(down)]
    taker = 1 - x % 2
    targets = [(h * 8 + z * 2 + taker, row) for h in (0, 1)]
    first, second = 1 - core, 3 - core
    sources = [(col, first * 4 + y), (col, second * 4 + y)]

    barrier = pltpu.get_barrier_semaphore()
    for device in line + sides + ring + [sibling] + sources:
        pl.semaphore_signal(barrier, inc=1, device_id=device, device_id_type=MESH)
    pl.semaphore_wait(barrier, 10)

    sent = []

    def send(src, dst, sem, device):
        copy = pltpu.make_async_remote_copy(
            src_ref=src,
            dst_ref=dst,
            send_sem=send_sem.at[len(sent)],
            recv_sem=sem,
            device_id=device,
            device_id_type=MESH,
        )
        copy.start()
        sent.append(copy)

    def send_row(slot, device, src=None):
        send(rows.at[slot] if src is None else src, rows.at[slot], row_sem.at[slot], device)

    def send_col(slot, device, src=None):
        send(cols.at[slot] if src is None else src, cols.at[slot], col_sem.at[slot], device)

    def wait(buffer, sem, slot):
        pltpu.make_async_remote_copy(
            src_ref=buffer.at[slot],
            dst_ref=buffer.at[slot],
            send_sem=send_sem.at[0],
            recv_sem=sem.at[slot],
            device_id=sibling,
            device_id_type=MESH,
        ).wait_recv()

    def wait_row(slot):
        wait(rows, row_sem, slot)

    def wait_col(slot):
        wait(cols, col_sem, slot)

    def row_slot(x_of, z_back):
        return x_of * 4 + (z + 4 - z_back) % 4

    for target in targets:
        send_col(col, target, own)
    for side in sides:
        send_row(col, side, own)
    for device in line:
        send_row(col, device, own)
    rows[col] = own[...]

    def pass_line(s):
        slot = row_slot(x, s)
        wait_row(slot)
        for side in sides:
            send_row(slot, side)

    def relay(x_from, side, s):
        slot = row_slot(x_from, s)
        wait_row(slot)
        send_row(slot, side)

    def col_slot(x_of, y_of):
        return x_of * 4 + y_of

    pass_line(1)
    for x_of in (first, second):
        slot = col_slot(x_of, y)
        wait_col(slot)
        for device in ring:
            send_col(slot, device)
        send_col(slot, sibling)
    relay(left, sides[0], 0)
    relay(right, sides[1], 1)
    pass_line(2)
    for x_of, y_of, device in ((first, down, ring[0]), (second, up, ring[1])):
        slot = col_slot(x_of, y_of)
        wait_col(slot)
        send_col(slot, device)
        send_col(slot, sibling)
    pass_line(3)
    for x_of, y_of in ((first, up), (second, down)):
        slot = col_slot(x_of, y_of)
        wait_col(slot)
        send_col(slot, sibling)
    relay(left, sides[0], 2)
    for x_of in (first, second):
        slot = col_slot(x_of, (y + 2) % 4)
        wait_col(slot)
        send_col(slot, sibling)
    relay(right, sides[1], 3)
    for x_of in (core, core + 2):
        for y_of in range(4):
            wait_col(col_slot(x_of, y_of))

    steps = rows.shape[2]

    def product(group):
        left_rows = rows[pl.ds(group * 4, 4)].reshape(256, steps)

        def tile(n, carry):
            right_rows = cols[pl.ds(n * 4, 4)].reshape(256, steps)
            block = lax.dot_general(
                left_rows,
                right_rows,
                (((1,), (1,)), ((), ())),
                preferred_element_type=jnp.float32,
            )
            out[pl.ds(group * 256, 256), pl.ds(pl.multiple_of(n * 256, 256), 256)] = block
            return carry

        lax.fori_loop(0, 4, tile, 0)

    far = (x + 2) % 4

    product(x)
    wait_row(row_slot(left, 1))
    wait_row(row_slot(left, 3))
    product(left)
    wait_row(row_slot(right, 0))
    wait_row(row_slot(right, 2))
    product(right)
    for s in range(4):
        wait_row(row_slot(far, s))
    product(far)
    for copy in sent:
        copy.wait_send()


def on_device(series, lengths, starts):
    normed = normalize(series, lengths, starts)
    pieces, steps = normed.shape
    shape = (16, pieces, steps)
    return pl.pallas_call(
        exchange,
        out_shape=jax.ShapeDtypeStruct((1024, 1024), jnp.float32),
        in_specs=[pl.BlockSpec(memory_space=pltpu.VMEM)],
        out_specs=pl.BlockSpec(memory_space=pltpu.VMEM),
        scratch_shapes=[
            pltpu.VMEM(shape, jnp.bfloat16),
            pltpu.VMEM(shape, jnp.bfloat16),
            pltpu.SemaphoreType.DMA((31,)),
            pltpu.SemaphoreType.DMA((16,)),
            pltpu.SemaphoreType.DMA((16,)),
        ],
        compiler_params=pltpu.CompilerParams(
            collective_id=0, has_side_effects=True, vmem_limit_bytes=40 * 1024 * 1024
        ),
        name="exchange",
    )(normed)


def solution(mesh):
    placed = (P(("row", "col"), None), P(("row", "col")), P(("row", "col")))
    return jax.shard_map(
        on_device, mesh=mesh, in_specs=placed, out_specs=P("row", "col"), check_vma=False
    )
```

time: 268 us -> 88 us (0.33)
  the two profiles are of different devices: /device:TPU:1 before, /device:TPU:204 now
where the time goes in v1:
time: 88 us; the launch traced here: 87.8 us
  Pallas kernels  79.4 us (90%)
  other arithmetic  6.31 us (7%)
  local copies, waits for them, and re-layouts  2.02 us (2%)
    pallas_call x1, Pallas kernels, on_device(): pl.pallas_call(exchange, out_shape=jax.ShapeDtypeStruct((1024, 1024), jnp...  79.4 us
    unnamed x1, local copies, waits for them, and re-layouts  2.02 us

profile of v1, /device:TPU:204, one launch (start us, length us, event | category | flops | bytes accessed | tf_op | source)
XLA Modules:
  0.0 87.8 jit_solution(5737284044828658193)
XLA Ops:
  0.0 0.7 add.10
  0.7 1.4 %select_reduce_fusion = f32[64]{0:T(128)S(1)} fusion(f32[64,2048]{1,0:T(8,128)} %param.3, s32[64]{0:T(128)S(1)} %add.10, s32[64]{0:T(128)} %param.5), kind=kLoop, calls=%fused_computation.3 | loop fusion | flops 655296 | bytes 525056 | tf_op jit(solution)/shard_map/reduce_sum | solution.py:17
  2.0 0.7 convert_divide_fusion.1
  2.7 1.5 %multiply_reduce_fusion = f32[64]{0:T(128)S(1)} fusion(f32[64,2048]{1,0:T(8,128)} %param.3, f32[64]{0:T(128)S(1)} %convert_divide_fusion.1, s32[64]{0:T(128)S(1)} %add.10, s32[64]{0:T(128)} %param.5), kind=kLoop, calls=%fused_computation.1 | loop fusion | flops 917440 | bytes 525312 | tf_op jit(solution)/shard_map/reduce_sum | solution.py:19
  4.2 0.7 multiply_sqrt_fusion
  4.9 1.4 %divide_convert_fusion.own = bf16[64,2048]{1,0:T(8,128)(2,1)S(1)} fusion(f32[64,2048]{1,0:T(8,128)} %param.3, f32[64]{0:T(128)S(1)} %multiply_sqrt_fusion, f32[64]{0:T(128)S(1)} %convert_divide_fusion.1, s32[64]{0:T(128)S(1)} %add.10, s32[64]{0:T(128)} %param.5), kind=kLoop, calls=%fused_computation | loop fusion | flops 917504 | bytes 787456 | tf_op jit(solution)/shard_map/convert_element_type | solution.py:20
  6.3 79.4 %exchange.1 = f32[1024,1024]{1,0:T(8,128)S(1)} custom-call(bf16[64,2048]{1,0:T(8,128)(2,1)S(1)} %divide_convert_fusion.own), custom_call_target="tpu_custom_call" | custom-call | tf_op jit(solution)/shard_map/exchange/pallas_call | solution.py:179
  85.8 2.0 %copy.5 = f32[1024,1024]{1,0:T(8,128)} copy(f32[1024,1024]{1,0:T(8,128)S(1)} %exchange.1) | data formatting | bytes 8388608

commit v2 on v0

v2 whole, which is shorter than its diff:
```python
import functools

import jax
import jax.numpy as jnp
from jax import lax
from jax.experimental import pallas as pl
from jax.experimental.pallas import tpu as pltpu
from jax.sharding import PartitionSpec as P

MESH = pl.DeviceIdType.MESH


def normalize(series, lengths, starts, normed):
    count, steps = series.shape
    diagonal = lax.broadcasted_iota(jnp.int32, (count, count), 0) == lax.broadcasted_iota(
        jnp.int32, (count, count), 1
    )

    def column(values):
        spread = jnp.where(diagonal, jnp.broadcast_to(values[...], (count, count)), 0)
        return jnp.sum(spread, axis=1, keepdims=True)

    valid, first = column(lengths), column(starts)
    positions = lax.broadcasted_iota(jnp.int32, (count, steps), 1)
    inside = ((positions >= first) & (positions < first + valid)).astype(jnp.float32)
    valid_count = valid.astype(jnp.float32)
    average = jnp.sum(inside * series[...], axis=1, keepdims=True) / valid_count
    centered = inside * (series[...] - average)
    variance = jnp.sum(centered * centered, axis=1, keepdims=True) / valid_count
    normed[...] = (centered / jnp.sqrt(valid_count * (variance + 1e-06))).astype(jnp.bfloat16)


PARTS = 2
COPIES = 120
FIRST = ["o", "x", "c"]
ORDER = (
    ("l1", "l2.m", "p", "h0", "l3.m", "l2.e", "h1", "f", "l3.e", "h2", "y", "h3", "v", "A", "B")
    + ("w", "C", "D")
)


def exchange(own, out, rows, cols, passing, send_sem, row_sem, col_sem, passing_sem):
    row, col = lax.axis_index("row"), lax.axis_index("col")
    half, y, core = row // 8, (row // 2) % 4, row % 2
    x, z = col // 4, col % 4
    right, left = (x + 1) % 4, (x + 3) % 4
    up, down = (y + 1) % 4, (y + 3) % 4

    def at_col(x_to, z_to):
        return (row, x_to * 4 + z_to)

    def at_y(y_to):
        return (half * 8 + y_to * 2 + core, col)

    sibling = (row + 1 - 2 * core, col)
    heights = [z, z + 1 - 2 * (z % 2), 2 - z // 2, 3 - 3 * (z // 2)]
    middle = z * (3 - z) // 2
    partner = at_col(x, heights[1])
    across = at_col(x, (3 - z) % 4)
    sides = [at_col(right, z), at_col(left, z)]
    ring = [at_y(up), at_y(down)]
    shift = 2 * (x % 2) + z // 2
    carrier = at_y((y + shift) % 4)
    moves = (shift + 3) // 4
    source = at_y((y + 4 - shift) % 4)
    theirs = half * 8 + ((y + 4 - shift) % 4) * 2 + core
    targets = [(h * 8 + y * 2 + 1 - z % 2, theirs) for h in (0, 1)]
    origin = (col // 2) % 4

    def places(y_of, height):
        turn = (y_of + 4 - origin) % 4
        near = turn // 2 * 4 + turn % 2 * 2 + height
        return near, near + 8

    carriers = [
        (col // 8 * 8 + y * 2 + col % 2, place) for place in places(y, 1 - core)
    ]

    barrier = pltpu.get_barrier_semaphore()

    def greet(device):
        pl.semaphore_signal(barrier, inc=1, device_id=device, device_id_type=MESH)

    for device in [partner, sibling] + sides + ring + carriers:
        greet(device)
    pl.when(middle == 1)(functools.partial(greet, across))
    pl.when(moves == 1)(functools.partial(greet, source))
    pl.semaphore_wait(barrier, 8 + middle + moves)

    sent = []

    def both(a, b):
        return b if a is None else a if b is None else a * b

    def send(src, dst, sem, device, when=None):
        copy = pltpu.make_async_remote_copy(
            src_ref=src,
            dst_ref=dst,
            send_sem=send_sem.at[len(sent)],
            recv_sem=sem,
            device_id=device,
            device_id_type=MESH,
        )
        if when is None:
            copy.start()
        else:
            pl.when(when == 1)(copy.start)
        sent.append((copy, when))

    def mine(part):
        return own.at[pl.ds(part * (64 // PARTS), 64 // PARTS)]

    def send_row(slot, part, device, src=None, when=None):
        i = slot * PARTS + part
        send(rows.at[i] if src is None else src, rows.at[i], row_sem.at[i], device, when)

    def send_col(slot, part, device, when=None):
        i = slot * PARTS + part
        send(cols.at[i], cols.at[i], col_sem.at[i], device, when)

    def wait(buffer, sem, i, when=None):
        copy = pltpu.make_async_remote_copy(
            src_ref=buffer.at[i],
            dst_ref=buffer.at[i],
            send_sem=send_sem.at[0],
            recv_sem=sem.at[i],
            device_id=sibling,
            device_id_type=MESH,
        )
        if when is None:
            copy.wait_recv()
        else:
            pl.when(when == 1)(copy.wait_recv)

    def wait_row(slot, part, when=None):
        wait(rows, row_sem, slot * PARTS + part, when)

    def wait_col(slot, part, when=None):
        wait(cols, col_sem, slot * PARTS + part, when)

    def carry(src, part, when):
        i = col * PARTS + part
        for target in targets:
            send(src, cols.at[i], col_sem.at[i], target, when)

    def start(name):
        for part in range(PARTS):
            if name == "x":
                for side in sides:
                    send_row(col, part, side, mine(part))
            elif name == "c":
                send(mine(part), passing.at[part], passing_sem.at[part], carrier, moves)
                carry(mine(part), part, 1 - moves)
            else:
                send_row(col, part, partner, mine(part))
                send_row(col, part, across, mine(part), middle)

    for name in FIRST:
        start(name)
    rows[pl.ds(col * PARTS, PARTS)] = own[...].reshape(PARTS, 64 // PARTS, own.shape[1])

    def step(name):
        kind, k = name[0], int(name[1:2].strip(".") or 0)
        on = None if "." not in name else middle if name[-1] == "m" else 1 - middle
        for part in range(PARTS):
            onward = part < PARTS // 2
            if kind == "l":
                slot = x * 4 + heights[k]
                wait_row(slot, part, on)
                if "e" not in name:
                    send_row(slot, part, across if k == 1 else partner, None, middle)
                for side in sides:
                    send_row(slot, part, side, None, on)
            elif kind == "h":
                slot = (left if onward else right) * 4 + heights[k]
                wait_row(slot, part, on)
                send_row(slot, part, sides[0] if onward else sides[1], None, on)
            elif kind == "p":
                wait(passing, passing_sem, part, both(moves, on))
                carry(passing.at[part], part, both(moves, on))
            else:
                if kind == "f":
                    y_of, onto = y, ring
                elif kind == "y":
                    y_of, onto = (down, ring[:1]) if onward else (up, ring[1:])
                elif kind == "v":
                    y_of, onto = up if onward else down, []
                else:
                    y_of, onto = (y + 2) % 4, []
                for slot in places(y_of, 1 - core):
                    wait_col(slot, part, on)
                    for device in onto:
                        send_col(slot, part, device, on)
                    send_col(slot, part, sibling, on)

    steps = rows.shape[2]

    def tile(group, groups, y_of):
        count = 4 * groups * PARTS
        left_rows = rows[pl.ds(group * 4 * PARTS, count)].reshape(groups * 256, steps)
        near, beyond = places(y_of, 0)
        right_rows = jnp.concatenate(
            [cols[pl.ds(place * PARTS, 2 * PARTS)].reshape(128, steps) for place in (near, beyond)],
            axis=0,
        )
        block = lax.dot_general(
            left_rows, right_rows, (((1,), (1,)), ((), ())), preferred_element_type=jnp.float32
        )
        for k, place in enumerate((near, beyond)):
            at = pl.multiple_of(place * 64, 128)
            out[pl.ds(group * 256, groups * 256), pl.ds(at, 128)] = block[:, k * 128 : k * 128 + 128]

    def wait_siblings(y_of):
        for slot in places(y_of, core):
            for part in range(PARTS):
                wait_col(slot, part)

    def loop(count, body):
        def run(i, carry):
            body(i)
            return carry

        lax.fori_loop(0, count, run, 0)

    def multiply(name):
        if name == "A":
            wait_siblings(y)
            tile(x, 1, y)
        elif name == "B":
            wait_siblings(down)
            wait_siblings(up)
            for height in range(4):
                for part in range(PARTS):
                    wait_row((right if part < PARTS // 2 else left) * 4 + height, part)

            def body(i):
                j, k = (i + 1) // 3, (i + 1) % 3
                tile((x + j + j // 2) % 4, 1, (y + k + k // 2) % 4)

            loop(8, body)
        elif name == "C":
            for height in range(4):
                for part in range(PARTS):
                    wait_row((x + 2) % 4 * 4 + height, part)
            loop(3, lambda k: tile((x + 2) % 4, 1, (y + k + k // 2) % 4))
        else:
            wait_siblings((y + 2) % 4)
            loop(2, lambda i: tile(2 * i, 2, (y + 2) % 4))

    for name in ORDER:
        if name.isupper():
            multiply(name)
        else:
            step(name)
    for copy, when in sent:
        if when is None:
            copy.wait_send()
        else:
            pl.when(when == 1)(copy.wait_send)


def on_device(series, lengths, starts):
    pieces, steps = series.shape
    normed = pl.pallas_call(
        normalize,
        out_shape=jax.ShapeDtypeStruct(series.shape, jnp.bfloat16),
        in_specs=[pl.BlockSpec(memory_space=pltpu.VMEM)] * 3,
        out_specs=pl.BlockSpec(memory_space=pltpu.VMEM),
        compiler_params=pltpu.CompilerParams(vmem_limit_bytes=16 * 1024 * 1024),
        name="normalize",
    )(series, lengths.reshape(1, pieces), starts.reshape(1, pieces))
    part = pieces // PARTS
    shape = (16 * PARTS, part, steps)
    return pl.pallas_call(
        exchange,
        out_shape=jax.ShapeDtypeStruct((1024, 1024), jnp.float32),
        in_specs=[pl.BlockSpec(memory_space=pltpu.VMEM)],
        out_specs=pl.BlockSpec(memory_space=pltpu.VMEM),
        scratch_shapes=[
            pltpu.VMEM(shape, jnp.bfloat16),
            pltpu.VMEM(shape, jnp.bfloat16),
            pltpu.VMEM((PARTS, part, steps), jnp.bfloat16),
            pltpu.SemaphoreType.DMA((COPIES,)),
            pltpu.SemaphoreType.DMA((16 * PARTS,)),
            pltpu.SemaphoreType.DMA((16 * PARTS,)),
            pltpu.SemaphoreType.DMA((PARTS,)),
        ],
        compiler_params=pltpu.CompilerParams(
            collective_id=0, has_side_effects=True, vmem_limit_bytes=40 * 1024 * 1024
        ),
        name="exchange",
    )(normed)


def solution(mesh):
    placed = (P(("row", "col"), None), P(("row", "col")), P(("row", "col")))
    return jax.shard_map(
        on_device, mesh=mesh, in_specs=placed, out_specs=P("row", "col"), check_vma=False
    )
```

time: 268 us -> 63.5 us (0.24)
  waiting for transfers between devices: 158 us -> 0 us
  starting transfers between devices: 62 us -> 0 us
  Pallas kernels: 0 us -> 58.9 us
  between operations: 13.4 us -> 0.02 us
  blocking collectives: 12.9 us -> 0 us
  matrix products: 10 us -> 0 us
  other arithmetic: 6.31 us -> 0 us
    all_gather x1 -> x0, waiting for transfers between devices: 83.3 us -> none  [on_device(): lax.all_gather(normed, 'col', axis=0, tiled=True)]
    all_to_all x2 -> x0, waiting for transfers between devices: 74.5 us -> none  [the longest x1 41.4 us: from_everyone(): return lax.all_to_all(copies, axis, split_axis=0, concat_axis=0, tiled=True)]
    all_to_all x2 -> x0, starting transfers between devices: 61.9 us -> none  [the longest x1 50.3 us: on_device(): lax.all_to_all(outgoing, 'col', split_axis=0, concat_axis=0, tiled=True)]
    pallas_call x0 -> x2, Pallas kernels: none -> 58.9 us  [the longest x1 58.5 us: on_device(): pl.pallas_call(exchange, out_shape=jax.ShapeDtypeStruct((1024, 1024), jnp...]
    all_to_all x1 -> x0, blocking collectives: 12.9 us -> none  [from_everyone(): return lax.all_to_all(copies, axis, split_axis=0, concat_axis=0, tiled=True)]
    dot_general x1 -> x0, matrix products: 10 us -> none  [gram_block(): lax.dot_general(left_rows, right_rows, (((1,), (1,)), ((), ())), preferre...]
    unnamed x2 -> x7, local copies, waits for them, and re-layouts: 0.01 us -> 4.37 us
    reduce_sum x2 -> x0, other arithmetic: 2.88 us -> none  [the longest x1 1.52 us: normalize(): variance = jnp.sum(centered * centered, axis=1, keepdims=True) / valid_count]
  transfers between devices with their start and end apart: 3 -> 0, of which waited for: 3 -> 0; matrix products, arithmetic and copies ran while one was open for 1% -> 0% of each run, Pallas kernels for 0% -> 0%
where the time goes in v2:
time: 63.5 us; the launch traced here: 63.3 us
  Pallas kernels  58.9 us (93%)
  local copies, waits for them, and re-layouts  4.37 us (7%)
    pallas_call x1, Pallas kernels, on_device(): pl.pallas_call(exchange, out_shape=jax.ShapeDtypeStruct((1024, 1024), jnp...  58.5 us
    unnamed x7, local copies, waits for them, and re-layouts  4.37 us

profile of v2, /device:TPU:1, one launch (start us, length us, event | category | flops | bytes accessed | tf_op | source)
XLA Modules:
  0.0 63.3 jit_solution(6424350332983947392)
XLA Ops:
  0.0 0.0 copy-start
  0.0 1.0 %copy-done = f32[64,2048]{1,0:T(8,128)S(1)} copy-done((f32[64,2048]{1,0:T(8,128)S(1)}, f32[64,2048]{1,0:T(8,128)}, u32[]{:S(2)}) %copy-start) | copy-done | bytes 524312
  1.0 0.0 copy-start.1
  1.0 0.7 %copy-done.1 = s32[64]{0:T(128)S(1)} copy-done((s32[64]{0:T(128)S(1)}, s32[64]{0:T(128)}, u32[]{:S(2)}) %copy-start.1) | copy-done | bytes 280
  1.7 0.0 copy-start.2
  1.7 0.7 %copy-done.2 = s32[64]{0:T(128)S(1)} copy-done((s32[64]{0:T(128)S(1)}, s32[64]{0:T(128)}, u32[]{:S(2)}) %copy-start.2) | copy-done | bytes 280
  2.4 0.4 normalize.1.own
  2.8 58.5 %exchange.1 = f32[1024,1024]{1,0:T(8,128)S(1)} custom-call(bf16[64,2048]{1,0:T(8,128)(2,1)S(1)} %normalize.1.own), custom_call_target="tpu_custom_call" | custom-call | tf_op jit(solution)/shard_map/exchange/pallas_call | solution.py:274
  61.3 2.0 %copy.5 = f32[1024,1024]{1,0:T(8,128)} copy(f32[1024,1024]{1,0:T(8,128)S(1)} %exchange.1) | data formatting | bytes 8388608
Async XLA Ops:
  0.0 1.0 %copy-start = (f32[64,2048]{1,0:T(8,128)S(1)}, f32[64,2048]{1,0:T(8,128)}, u32[]{:S(2)}) copy-start(f32[64,2048]{1,0:T(8,128)} %series.1) | copy-start | bytes 1572868
  1.0 0.7 %copy-start.1 = (s32[64]{0:T(128)S(1)}, s32[64]{0:T(128)}, u32[]{:S(2)}) copy-start(s32[64]{0:T(128)} %param.4) | copy-start | bytes 772
  1.7 0.7 %copy-start.2 = (s32[64]{0:T(128)S(1)}, s32[64]{0:T(128)}, u32[]{:S(2)}) copy-start(s32[64]{0:T(128)} %param.5) | copy-start | bytes 772

commit v3 on v2

--- a/solution.py
+++ b/solution.py
@@ -10,7 +10,7 @@
 MESH = pl.DeviceIdType.MESH
 
 
-def normalize(series, lengths, starts, normed):
+def normalize(series, lengths, starts):
     count, steps = series.shape
     diagonal = lax.broadcasted_iota(jnp.int32, (count, count), 0) == lax.broadcasted_iota(
         jnp.int32, (count, count), 1
@@ -27,19 +27,22 @@
     average = jnp.sum(inside * series[...], axis=1, keepdims=True) / valid_count
     centered = inside * (series[...] - average)
     variance = jnp.sum(centered * centered, axis=1, keepdims=True) / valid_count
-    normed[...] = (centered / jnp.sqrt(valid_count * (variance + 1e-06))).astype(jnp.bfloat16)
+    return (centered / jnp.sqrt(valid_count * (variance + 1e-06))).astype(jnp.bfloat16)
 
 
 PARTS = 2
-COPIES = 120
+COPIES = 140
+SHORT = 1
 FIRST = ["o", "x", "c"]
 ORDER = (
-    ("l1", "l2.m", "p", "h0", "l3.m", "l2.e", "h1", "f", "l3.e", "h2", "y", "h3", "v", "A", "B")
-    + ("w", "C", "D")
+    ("p", "l1", "l2.m", "h0", "h1", "f", "l3.m", "l2.e", "l3.e", "h2", "y", "q", "v", "w", "h3")
+    + ("A", "B", "C", "D")
 )
 
 
-def exchange(own, out, rows, cols, passing, send_sem, row_sem, col_sem, passing_sem):
+def exchange(series_in, lengths_in, starts_in, out, *scratch):
+    series, lengths, starts, own, rows, cols, passing = scratch[:7]
+    send_sem, row_sem, col_sem, passing_sem, in_sem = scratch[7:]
     row, col = lax.axis_index("row"), lax.axis_index("col")
     half, y, core = row // 8, (row // 2) % 4, row % 2
     x, z = col // 4, col % 4
@@ -76,6 +79,14 @@
         (col // 8 * 8 + y * 2 + col % 2, place) for place in places(y, 1 - core)
     ]
 
+    loads = [
+        pltpu.make_async_copy(src, dst, in_sem.at[i])
+        for i, (src, dst) in enumerate(
+            ((series_in, series), (lengths_in, lengths), (starts_in, starts))
+        )
+    ]
+    for load in loads:
+        load.start()
     barrier = pltpu.get_barrier_semaphore()
 
     def greet(device):
@@ -85,6 +96,11 @@
         greet(device)
     pl.when(middle == 1)(functools.partial(greet, across))
     pl.when(moves == 1)(functools.partial(greet, source))
+    for load in loads:
+        load.wait()
+    normed = normalize(series, lengths, starts)
+    own[...] = normed
+    rows[pl.ds(col * PARTS, PARTS)] = normed.reshape(PARTS, 64 // PARTS, own.shape[1])
     pl.semaphore_wait(barrier, 8 + middle + moves)
 
     sent = []
@@ -157,7 +173,6 @@
 
     for name in FIRST:
         start(name)
-    rows[pl.ds(col * PARTS, PARTS)] = own[...].reshape(PARTS, 64 // PARTS, own.shape[1])
 
     def step(name):
         kind, k = name[0], int(name[1:2].strip(".") or 0)
@@ -169,8 +184,15 @@
                 wait_row(slot, part, on)
                 if "e" not in name:
                     send_row(slot, part, across if k == 1 else partner, None, middle)
-                for side in sides:
+                one_way = k == 1 or (k == 2 and SHORT and "m" in name)
+                for side in (sides[:1] if onward else sides[1:]) if one_way else sides:
                     send_row(slot, part, side, None, on)
+            elif kind == "q":
+                slot = (right if onward else left) * 4 + z
+                wait_row(slot, part, on)
+                send_row(slot, part, partner, None, on)
+                if SHORT:
+                    send_row(slot, part, across, None, middle if on is None or "m" in name else 0 * z)
             elif kind == "h":
                 slot = (left if onward else right) * 4 + heights[k]
                 wait_row(slot, part, on)
@@ -229,7 +251,7 @@
         elif name == "B":
             wait_siblings(down)
             wait_siblings(up)
-            for height in range(4):
+            for height in heights[1:]:
                 for part in range(PARTS):
                     wait_row((right if part < PARTS // 2 else left) * 4 + height, part)
 
@@ -261,22 +283,18 @@
 
 def on_device(series, lengths, starts):
     pieces, steps = series.shape
-    normed = pl.pallas_call(
-        normalize,
-        out_shape=jax.ShapeDtypeStruct(series.shape, jnp.bfloat16),
-        in_specs=[pl.BlockSpec(memory_space=pltpu.VMEM)] * 3,
-        out_specs=pl.BlockSpec(memory_space=pltpu.VMEM),
-        compiler_params=pltpu.CompilerParams(vmem_limit_bytes=16 * 1024 * 1024),
-        name="normalize",
-    )(series, lengths.reshape(1, pieces), starts.reshape(1, pieces))
     part = pieces // PARTS
     shape = (16 * PARTS, part, steps)
     return pl.pallas_call(
         exchange,
         out_shape=jax.ShapeDtypeStruct((1024, 1024), jnp.float32),
-        in_specs=[pl.BlockSpec(memory_space=pltpu.VMEM)],
+        in_specs=[pl.BlockSpec(memory_space=pltpu.HBM)] * 3,
         out_specs=pl.BlockSpec(memory_space=pltpu.VMEM),
         scratch_shapes=[
+            pltpu.VMEM((pieces, steps), jnp.float32),
+            pltpu.VMEM((1, pieces), jnp.int32),
+            pltpu.VMEM((1, pieces), jnp.int32),
+            pltpu.VMEM((pieces, steps), jnp.bfloat16),
             pltpu.VMEM(shape, jnp.bfloat16),
             pltpu.VMEM(shape, jnp.bfloat16),
             pltpu.VMEM((PARTS, part, steps), jnp.bfloat16),
@@ -284,12 +302,13 @@
             pltpu.SemaphoreType.DMA((16 * PARTS,)),
             pltpu.SemaphoreType.DMA((16 * PARTS,)),
             pltpu.SemaphoreType.DMA((PARTS,)),
+            pltpu.SemaphoreType.DMA((3,)),
         ],
         compiler_params=pltpu.CompilerParams(
             collective_id=0, has_side_effects=True, vmem_limit_bytes=40 * 1024 * 1024
         ),
         name="exchange",
-    )(normed)
+    )(series, lengths.reshape(1, pieces), starts.reshape(1, pieces))
 
 
 def solution(mesh):

time: 63.5 us -> 61.5 us (0.969); the launches traced: 63.3 us -> 60.5 us
  Pallas kernels: 58.9 us -> 56.1 us
    pallas_call x1, Pallas kernels: 58.5 us -> 56.1 us  [on_device(): pl.pallas_call(exchange, out_shape=jax.ShapeDtypeStruct((1024, 1024), jnp...]
where the time goes in v3:
time: 61.5 us; the launch traced here: 60.5 us
  Pallas kernels  56.1 us (91%)
  local copies, waits for them, and re-layouts  4.37 us (7%)
    pallas_call x1, Pallas kernels, on_device(): pl.pallas_call(exchange, out_shape=jax.ShapeDtypeStruct((1024, 1024), jnp...  56.1 us
    unnamed x7, local copies, waits for them, and re-layouts  4.37 us

profile of v3, /device:TPU:1, one launch (start us, length us, event | category | flops | bytes accessed | tf_op | source)
XLA Modules:
  0.0 60.5 jit_solution(10091358382244746093)
XLA Ops:
  0.0 0.0 copy-start
  0.0 1.0 %copy-done = f32[64,2048]{1,0:T(8,128)S(1)} copy-done((f32[64,2048]{1,0:T(8,128)S(1)}, f32[64,2048]{1,0:T(8,128)}, u32[]{:S(2)}) %copy-start) | copy-done | bytes 524312
  1.0 0.0 copy-start.1
  1.0 0.7 %copy-done.1 = s32[64]{0:T(128)S(1)} copy-done((s32[64]{0:T(128)S(1)}, s32[64]{0:T(128)}, u32[]{:S(2)}) %copy-start.1) | copy-done | bytes 280
  1.7 0.0 copy-start.2
  1.7 0.7 %copy-done.2 = s32[64]{0:T(128)S(1)} copy-done((s32[64]{0:T(128)S(1)}, s32[64]{0:T(128)}, u32[]{:S(2)}) %copy-start.2) | copy-done | bytes 280
  2.4 56.1 %exchange.1 = f32[1024,1024]{1,0:T(8,128)S(1)} custom-call(f32[64,2048]{1,0:T(8,128)S(1)} %copy-done, s32[1,64]{1,0:T(1,128)S(1)} %bitcast.2, s32[1,64]{1,0:T(1,128)S(1)} %bitcast.3), custom_call_target="tpu_custom_call" | custom-call | tf_op jit(solution)/shard_map/exchange/pallas_call | solution.py:288
  58.4 2.0 %copy.5 = f32[1024,1024]{1,0:T(8,128)} copy(f32[1024,1024]{1,0:T(8,128)S(1)} %exchange.1) | data formatting | bytes 8388608
Async XLA Ops:
  0.0 1.0 %copy-start = (f32[64,2048]{1,0:T(8,128)S(1)}, f32[64,2048]{1,0:T(8,128)}, u32[]{:S(2)}) copy-start(f32[64,2048]{1,0:T(8,128)} %series_in.1) | copy-start | bytes 1572868
  1.0 0.7 %copy-start.1 = (s32[64]{0:T(128)S(1)}, s32[64]{0:T(128)}, u32[]{:S(2)}) copy-start(s32[64]{0:T(128)} %param.4) | copy-start | bytes 772
  1.7 0.7 %copy-start.2 = (s32[64]{0:T(128)S(1)}, s32[64]{0:T(128)}, u32[]{:S(2)}) copy-start(s32[64]{0:T(128)} %param.5) | copy-start | bytes 772

commit v4 on v3

--- a/solution.py
+++ b/solution.py
@@ -10,17 +10,16 @@
 MESH = pl.DeviceIdType.MESH
 
 
-def normalize(series, lengths, starts):
+def normalize(series, windows):
     count, steps = series.shape
-    diagonal = lax.broadcasted_iota(jnp.int32, (count, count), 0) == lax.broadcasted_iota(
-        jnp.int32, (count, count), 1
-    )
-
-    def column(values):
-        spread = jnp.where(diagonal, jnp.broadcast_to(values[...], (count, count)), 0)
-        return jnp.sum(spread, axis=1, keepdims=True)
-
-    valid, first = column(lengths), column(starts)
+    lane = lax.broadcasted_iota(jnp.int32, (count, 2 * count), 1)
+    series_of = lax.broadcasted_iota(jnp.int32, (count, 2 * count), 0)
+    spread = jnp.broadcast_to(windows[...], (count, 2 * count))
+
+    def column(first_lane):
+        return jnp.sum(jnp.where(lane == series_of + first_lane, spread, 0), axis=1, keepdims=True)
+
+    valid, first = column(0), column(count)
     positions = lax.broadcasted_iota(jnp.int32, (count, steps), 1)
     inside = ((positions >= first) & (positions < first + valid)).astype(jnp.float32)
     valid_count = valid.astype(jnp.float32)
@@ -35,14 +34,14 @@
 SHORT = 1
 FIRST = ["o", "x", "c"]
 ORDER = (
-    ("p", "l1", "l2.m", "h0", "h1", "f", "l3.m", "l2.e", "l3.e", "h2", "y", "q", "v", "w", "h3")
-    + ("A", "B", "C", "D")
+    ("p", "l1", "l2.m", "h0", "h1", "f", "l2.e", "l3.m", "l3.e", "h2", "y", "q", "v", "h3")
+    + ("A", "B", "w", "E", "C", "D")
 )
 
 
-def exchange(series_in, lengths_in, starts_in, out, *scratch):
-    series, lengths, starts, own, rows, cols, passing = scratch[:7]
-    send_sem, row_sem, col_sem, passing_sem, in_sem = scratch[7:]
+def exchange(series_in, windows_in, out, *scratch):
+    series, windows, own, rows, cols, passing = scratch[:6]
+    send_sem, row_sem, col_sem, passing_sem, in_sem = scratch[6:]
     row, col = lax.axis_index("row"), lax.axis_index("col")
     half, y, core = row // 8, (row // 2) % 4, row % 2
     x, z = col // 4, col % 4
@@ -82,7 +81,7 @@
     loads = [
         pltpu.make_async_copy(src, dst, in_sem.at[i])
         for i, (src, dst) in enumerate(
-            ((series_in, series), (lengths_in, lengths), (starts_in, starts))
+            ((series_in, series), (windows_in, windows))
         )
     ]
     for load in loads:
@@ -98,7 +97,7 @@
     pl.when(moves == 1)(functools.partial(greet, source))
     for load in loads:
         load.wait()
-    normed = normalize(series, lengths, starts)
+    normed = normalize(series, windows)
     own[...] = normed
     rows[pl.ds(col * PARTS, PARTS)] = normed.reshape(PARTS, 64 // PARTS, own.shape[1])
     pl.semaphore_wait(barrier, 8 + middle + moves)
@@ -217,18 +216,17 @@
 
     steps = rows.shape[2]
 
-    def tile(group, groups, y_of):
+    def tile(group, groups, *y_from):
         count = 4 * groups * PARTS
         left_rows = rows[pl.ds(group * 4 * PARTS, count)].reshape(groups * 256, steps)
-        near, beyond = places(y_of, 0)
+        blocks = [place for y_of in y_from for place in places(y_of, 0)]
         right_rows = jnp.concatenate(
-            [cols[pl.ds(place * PARTS, 2 * PARTS)].reshape(128, steps) for place in (near, beyond)],
-            axis=0,
+            [cols[pl.ds(place * PARTS, 2 * PARTS)].reshape(128, steps) for place in blocks], axis=0
         )
         block = lax.dot_general(
             left_rows, right_rows, (((1,), (1,)), ((), ())), preferred_element_type=jnp.float32
         )
-        for k, place in enumerate((near, beyond)):
+        for k, place in enumerate(blocks):
             at = pl.multiple_of(place * 64, 128)
             out[pl.ds(group * 256, groups * 256), pl.ds(at, 128)] = block[:, k * 128 : k * 128 + 128]
 
@@ -249,25 +247,22 @@
             wait_siblings(y)
             tile(x, 1, y)
         elif name == "B":
-            wait_siblings(down)
-            wait_siblings(up)
             for height in heights[1:]:
                 for part in range(PARTS):
                     wait_row((right if part < PARTS // 2 else left) * 4 + height, part)
-
-            def body(i):
-                j, k = (i + 1) // 3, (i + 1) % 3
-                tile((x + j + j // 2) % 4, 1, (y + k + k // 2) % 4)
-
-            loop(8, body)
+            loop(2, lambda i: tile((x + 1 + 2 * i) % 4, 1, y))
+        elif name == "E":
+            wait_siblings(down)
+            wait_siblings(up)
+            loop(3, lambda i: tile((x + i + i // 2) % 4, 1, down, up))
         elif name == "C":
             for height in range(4):
                 for part in range(PARTS):
                     wait_row((x + 2) % 4 * 4 + height, part)
-            loop(3, lambda k: tile((x + 2) % 4, 1, (y + k + k // 2) % 4))
+            tile((x + 2) % 4, 1, y, down, up)
         else:
             wait_siblings((y + 2) % 4)
-            loop(2, lambda i: tile(2 * i, 2, (y + 2) % 4))
+            tile(0, 4, (y + 2) % 4)
 
     for name in ORDER:
         if name.isupper():
@@ -283,17 +278,17 @@
 
 def on_device(series, lengths, starts):
     pieces, steps = series.shape
+    windows = jnp.concatenate([lengths, starts]).reshape(1, 2 * pieces)
     part = pieces // PARTS
     shape = (16 * PARTS, part, steps)
     return pl.pallas_call(
         exchange,
         out_shape=jax.ShapeDtypeStruct((1024, 1024), jnp.float32),
-        in_specs=[pl.BlockSpec(memory_space=pltpu.HBM)] * 3,
+        in_specs=[pl.BlockSpec(memory_space=pltpu.HBM)] * 2,
         out_specs=pl.BlockSpec(memory_space=pltpu.VMEM),
         scratch_shapes=[
             pltpu.VMEM((pieces, steps), jnp.float32),
-            pltpu.VMEM((1, pieces), jnp.int32),
-            pltpu.VMEM((1, pieces), jnp.int32),
+            pltpu.VMEM((1, 2 * pieces), jnp.int32),
             pltpu.VMEM((pieces, steps), jnp.bfloat16),
             pltpu.VMEM(shape, jnp.bfloat16),
             pltpu.VMEM(shape, jnp.bfloat16),
@@ -302,13 +297,13 @@
             pltpu.SemaphoreType.DMA((16 * PARTS,)),
             pltpu.SemaphoreType.DMA((16 * PARTS,)),
             pltpu.SemaphoreType.DMA((PARTS,)),
-            pltpu.SemaphoreType.DMA((3,)),
+            pltpu.SemaphoreType.DMA((2,)),
         ],
         compiler_params=pltpu.CompilerParams(
             collective_id=0, has_side_effects=True, vmem_limit_bytes=40 * 1024 * 1024
         ),
         name="exchange",
-    )(series, lengths.reshape(1, pieces), starts.reshape(1, pieces))
+    )(series, windows)
 
 
 def solution(mesh):

time: 61.5 us -> 59.9 us (0.974); the launches traced: 60.5 us -> 59.8 us
  local copies, waits for them, and re-layouts: 4.37 us -> 3.06 us
  other arithmetic: 0 us -> 0.75 us
    unnamed x7 -> x3, local copies, waits for them, and re-layouts: 4.37 us -> 3.06 us
    reshape x0 -> x1, other arithmetic: none -> 0.75 us  [on_device(): windows = jnp.concatenate([lengths, starts]).reshape(1, 2 * pieces)]
where the time goes in v4:
time: 59.9 us; the launch traced here: 59.8 us
  Pallas kernels  56 us (93%)
  local copies, waits for them, and re-layouts  3.06 us (5%)
  other arithmetic  0.75 us (1%)
    pallas_call x1, Pallas kernels, on_device(): pl.pallas_call(exchange, out_shape=jax.ShapeDtypeStruct((1024, 1024), jnp...  56 us
    unnamed x3, local copies, waits for them, and re-layouts  3.06 us

profile of v4, /device:TPU:1, one launch (start us, length us, event | category | flops | bytes accessed | tf_op | source)
XLA Modules:
  0.0 59.8 jit_solution(5358392142048397597)
XLA Ops:
  0.0 0.7 %add_bitcast_fusion.windows_in = s32[1,128]{1,0:T(1,128)S(1)} fusion(s32[64]{0:T(128)} %param.5, s32[64]{0:T(128)} %param.4), kind=kLoop, calls=%fused_computation | loop fusion | flops 128 | bytes 1024 | tf_op jit(solution)/shard_map/reshape | solution.py:281
  0.7 0.0 copy-start
  0.7 1.0 %copy-done = f32[64,2048]{1,0:T(8,128)S(1)} copy-done((f32[64,2048]{1,0:T(8,128)S(1)}, f32[64,2048]{1,0:T(8,128)}, u32[]{:S(2)}) %copy-start) | copy-done | bytes 524312
  1.8 56.0 %exchange.1 = f32[1024,1024]{1,0:T(8,128)S(1)} custom-call(f32[64,2048]{1,0:T(8,128)S(1)} %copy-done, s32[1,128]{1,0:T(1,128)S(1)} %add_bitcast_fusion.windows_in), custom_call_target="tpu_custom_call" | custom-call | tf_op jit(solution)/shard_map/exchange/pallas_call | solution.py:284
  57.8 2.0 %copy.5 = f32[1024,1024]{1,0:T(8,128)} copy(f32[1024,1024]{1,0:T(8,128)S(1)} %exchange.1) | data formatting | bytes 8388608
Async XLA Ops:
  0.7 1.0 %copy-start = (f32[64,2048]{1,0:T(8,128)S(1)}, f32[64,2048]{1,0:T(8,128)}, u32[]{:S(2)}) copy-start(f32[64,2048]{1,0:T(8,128)} %series_in.1) | copy-start | bytes 1572868

commit v5 on v4

--- a/solution.py
+++ b/solution.py
@@ -31,7 +31,6 @@
 
 PARTS = 2
 COPIES = 140
-SHORT = 1
 FIRST = ["o", "x", "c"]
 ORDER = (
     ("p", "l1", "l2.m", "h0", "h1", "f", "l2.e", "l3.m", "l3.e", "h2", "y", "q", "v", "h3")
@@ -66,7 +65,7 @@
     moves = (shift + 3) // 4
     source = at_y((y + 4 - shift) % 4)
     theirs = half * 8 + ((y + 4 - shift) % 4) * 2 + core
-    targets = [(h * 8 + y * 2 + 1 - z % 2, theirs) for h in (0, 1)]
+    targets = [(h * 8 + y * 2 + 1 - z % 2, theirs) for h in (1 - half, half)]
     origin = (col // 2) % 4
 
     def places(y_of, height):
@@ -183,15 +182,13 @@
                 wait_row(slot, part, on)
                 if "e" not in name:
                     send_row(slot, part, across if k == 1 else partner, None, middle)
-                one_way = k == 1 or (k == 2 and SHORT and "m" in name)
+                one_way = k == 1
                 for side in (sides[:1] if onward else sides[1:]) if one_way else sides:
                     send_row(slot, part, side, None, on)
             elif kind == "q":
                 slot = (right if onward else left) * 4 + z
                 wait_row(slot, part, on)
                 send_row(slot, part, partner, None, on)
-                if SHORT:
-                    send_row(slot, part, across, None, middle if on is None or "m" in name else 0 * z)
             elif kind == "h":
                 slot = (left if onward else right) * 4 + heights[k]
                 wait_row(slot, part, on)

time: 59.9 us -> 59.9 us (level)
  no operation moved by 1% of the time
where the time goes in v5:
time: 59.9 us; the launch traced here: 59.8 us
  Pallas kernels  56 us (93%)
  local copies, waits for them, and re-layouts  3.06 us (5%)
  other arithmetic  0.75 us (1%)
    pallas_call x1, Pallas kernels, on_device(): pl.pallas_call(exchange, out_shape=jax.ShapeDtypeStruct((1024, 1024), jnp...  56 us
    unnamed x3, local copies, waits for them, and re-layouts  3.06 us

profile of v5, /device:TPU:1, one launch (start us, length us, event | category | flops | bytes accessed | tf_op | source)
XLA Modules:
  0.0 59.8 jit_solution(1411066480460297229)
XLA Ops:
  0.0 0.7 %add_bitcast_fusion.windows_in = s32[1,128]{1,0:T(1,128)S(1)} fusion(s32[64]{0:T(128)} %param.5, s32[64]{0:T(128)} %param.4), kind=kLoop, calls=%fused_computation | loop fusion | flops 128 | bytes 1024 | tf_op jit(solution)/shard_map/reshape | solution.py:278
  0.7 0.0 copy-start
  0.7 1.0 %copy-done = f32[64,2048]{1,0:T(8,128)S(1)} copy-done((f32[64,2048]{1,0:T(8,128)S(1)}, f32[64,2048]{1,0:T(8,128)}, u32[]{:S(2)}) %copy-start) | copy-done | bytes 524312
  1.8 56.0 %exchange.1 = f32[1024,1024]{1,0:T(8,128)S(1)} custom-call(f32[64,2048]{1,0:T(8,128)S(1)} %copy-done, s32[1,128]{1,0:T(1,128)S(1)} %add_bitcast_fusion.windows_in), custom_call_target="tpu_custom_call" | custom-call | tf_op jit(solution)/shard_map/exchange/pallas_call | solution.py:281
  57.8 2.0 %copy.5 = f32[1024,1024]{1,0:T(8,128)} copy(f32[1024,1024]{1,0:T(8,128)S(1)} %exchange.1) | data formatting | bytes 8388608
Async XLA Ops:
  0.7 1.0 %copy-start = (f32[64,2048]{1,0:T(8,128)S(1)}, f32[64,2048]{1,0:T(8,128)}, u32[]{:S(2)}) copy-start(f32[64,2048]{1,0:T(8,128)} %series_in.1) | copy-start | bytes 1572868
